TPU v7x, 128 devices: a whole 4x4x4 slice. The times are simulated.
128 devices in a mesh: gx: 8 (over y, core), gy: 16 (over z, x).
Axes of the slice: x: 4, y: 4, z: 4, core: 2. Of those that a mesh axis runs over, the one named last changes fastest.
Arguments:
- transfer: bfloat16 [2048, 75, 128], P(('gx', 'gy')), may hold values from -6 to 6
- positions: float32 [2048, 3, 128], P(('gx', 'gy')), may hold values from -4 to 4
- normals: float32 [2048, 3, 128], P(('gx', 'gy')), may hold values from -4 to 4
- area: float32 [2048, 128], P(('gx', 'gy')), may hold values from 0.06 to 3
- albedo: float32 [2048, 3, 128], P(('gx', 'gy')), may hold values from 0.3 to 0.9
- pairs: int32 [2048, 40], P(('gx', 'gy')), may hold values from 0 to 2047, as said below
- home: int32 [2048], replicated, may hold values from 0 to 2047, as said below
Outputs:
- bounce_one: bfloat16 [2048, 75, 128], P(('gx', 'gy'))
- bounce_two: bfloat16 [2048, 75, 128], P(('gx', 'gy'))
- energies: float32 [2], replicated
Inputs may be any that keep to these rules, and one draw needn't show every extreme that they name: `home`: A permutation; the block in slot s is held by device s // 16, devices counted gx major. `pairs`: the first 16 entries of a row name blocks held by the same device as the row's slot, the other 24 name blocks held by other devices. Over the rows of one device, the far entries name at most 2 distinct blocks of any one other device, and exactly 2 of some. Ids may repeat within a row; each entry counts.
All inputs are finite; a program needn't handle non-finite values.
Results may differ from a plain program's by a relative error of at most 0.02.
Values may be sent and summed in bfloat16 or wider, within the bound.
A program may use at most 128 MiB of HBM per device.

v0:
```python
import functools
import itertools

import jax
import jax.numpy as jnp
import numpy as np
from jax import lax
from jax.experimental import pallas as pl
from jax.experimental.pallas import tpu as pltpu
from jax.sharding import Mesh
from jax.sharding import PartitionSpec as P

AX = ("y", "c", "z", "x")
SZ = (4, 2, 4, 4)
NDEV = 128
SLOTS, NEAR, FAR, CH, V = 16, 16, 24, 75, 128
ROWS = 80
F32, BF16, I32 = jnp.float32, jnp.bfloat16, jnp.int32
MESH = pl.DeviceIdType.MESH


def rounded(t):
    return t.astype(BF16).astype(F32)


def pieces3(t):
    a = rounded(t)
    b = rounded(t - a)
    return a, b, rounded(t - a - b)


def rows_of(shape):
    return lax.broadcasted_iota(I32, shape, 0)


def source_features(v):
    r = rows_of((8, V))
    vh = rounded(v)
    vl = rounded(v - vh)
    m = -(v * v[6:7])
    mh = rounded(m)
    ml = rounded(m - mh)
    x = jnp.where(r < 3, v, 0.0)
    c = pieces3(jnp.sum(pltpu.roll(m, 5, 0) * x, axis=0, keepdims=True))
    e = pieces3(jnp.sum(x * x, axis=0, keepdims=True) + 1.0)
    cv = jnp.ones((8, V), F32)
    for i, row in enumerate(c + e):
        cv = jnp.where(r == i, row, cv)
    return jnp.concatenate([vh, vh, vl, mh, mh, ml, cv, jnp.zeros((8, V), F32)], axis=0).astype(BF16)


def receiver_features(v):
    r = rows_of((8, V))
    z = jnp.zeros((8, V), F32)
    x = jnp.where(r < 3, v, 0.0)
    n = jnp.where(r < 3, pltpu.roll(v, 5, 0), 0.0) * (1.0 / np.pi)
    nh = rounded(n)
    nl = rounded(n - nh)
    xh = rounded(x)
    xl = rounded(x - xh)
    k = pieces3(-jnp.sum(n * x, axis=0, keepdims=True))
    q = pieces3(jnp.sum(x * x, axis=0, keepdims=True))
    xh3 = -pltpu.roll(xh, 3, 0)
    xl3 = -pltpu.roll(xl, 3, 0)
    last = r == 7
    ap = [jnp.where(last, k[0], nh), jnp.where(last, k[1], nl), nh, z, z, z, jnp.where(r == 6, k[2], z), z]
    aq = [z, z, z, xh3, xl3, xh3, jnp.where(r < 3, 1.0, z), z]
    d = [jnp.where(last, q[0], -2.0 * xh), jnp.where(last, q[1], -2.0 * xl), -2.0 * xh, z, z, z,
         jnp.where((r >= 3) & (r < 6), 1.0, jnp.where(r == 6, q[2], z)), z]
    ap, aq, d = (jnp.concatenate(t, axis=0).astype(BF16) for t in (ap, aq, d))
    o = jnp.zeros((64, V), BF16)
    top = jnp.concatenate([ap, aq, o, o, d, o], axis=1)
    bottom = jnp.concatenate([o, o, ap, aq, o, d], axis=1)
    return jnp.concatenate([top, bottom], axis=0)


def pair_factors(feats, recv):
    out = lax.dot_general(feats, recv, (((0,), (0,)), ((), ())), preferred_element_type=F32)
    parts = []
    for i in range(2):
        ap = out[:, 256 * i : 256 * i + 128]
        aq = out[:, 256 * i + 128 : 256 * i + 256]
        d = out[:, 512 + 128 * i : 640 + 128 * i]
        parts.append((jnp.maximum(ap, 0.0) * jnp.maximum(aq, 0.0) / (d * d)).astype(BF16))
    return jnp.concatenate(parts, axis=0)


def me4():
    return tuple(lax.axis_index(a) for a in AX)


def my_index():
    y, c, z, x = me4()
    return ((y * 2 + c) * 4 + z) * 4 + x


def shifted(off):
    return tuple(lax.rem(i + o, s) for i, o, s in zip(me4(), off, SZ))


def flat(t):
    return ((t[0] * 2 + t[1]) * 4 + t[2]) * 4 + t[3]


def index_kernel(pairs_ref, home_ref, idx_ref, req_ref):
    p = pairs_ref[...]
    home = home_ref[...]
    shape = (SLOTS, V)
    lane = lax.broadcasted_iota(I32, shape, 1)
    low, high = p & 127, p >> 7
    slot = jnp.zeros(shape, I32)
    for h in range(16):
        got = jnp.take_along_axis(jnp.broadcast_to(home[h : h + 1], shape), low, axis=1)
        slot = jnp.where(high == h, got, slot)
    owner, local = slot >> 4, slot & 15
    lo = jnp.full(shape, 99, I32)
    hi = jnp.full(shape, -1, I32)
    for j in range(NEAR, NEAR + FAR):
        same = owner[:, j : j + 1] == lane
        lo = jnp.where(same, jnp.minimum(lo, local[:, j : j + 1]), lo)
        hi = jnp.where(same, jnp.maximum(hi, local[:, j : j + 1]), hi)
    lo = jnp.min(lo, axis=0, keepdims=True)
    hi = jnp.max(hi, axis=0, keepdims=True)
    lo = jnp.where(lo > 15, 0, lo)
    hi = jnp.where(hi < 0, 0, hi)
    first = jnp.take_along_axis(jnp.broadcast_to(lo, shape), owner, axis=1)
    far = owner * 2 + jnp.where(local != first, 1, 0)
    idx_ref[...] = jnp.where(lane < NEAR, local, far)
    req_ref[...] = jnp.where(rows_of((2, V)) == 0, lo, hi)


OFFSETS = [o for o in itertools.product(range(4), range(2), range(4), range(4)) if any(o)]
ORDER = [OFFSETS[i] for i in np.random.RandomState(0).permutation(len(OFFSETS))]


def send_all(src_of, dst, send_sem, recv_sem):
    mine = my_index()
    for off in ORDER:
        to = shifted(off)
        pltpu.make_async_remote_copy(
            src_of(flat(to)), dst.at[mine], send_sem, recv_sem, device_id=to, device_id_type=MESH
        ).start()


def wait_all(buf, sem):
    part = buf.at[pl.ds(0, NDEV - 1)]
    pltpu.make_async_copy(part, part, sem).wait()


def main_kernel(
    idx, req_ref, tr_ref, geo_ref, alb_ref, b1_ref, b2_ref, en_ref,
    reqall, wanted, en_all, near_s, near_g, send_g, recv_g, send_s, recv_s, recv_s2,
    feats, factors, acc, send_sem, recv_sem, local_sem,
):
    send_all(lambda d: req_ref, reqall, send_sem.at[0], recv_sem.at[0])
    reqall[my_index()] = req_ref[...]
    en_all[my_index()] = jnp.zeros((8, V), F32)
    near_s[:, 64:, :] = jnp.zeros((SLOTS, ROWS - 64, V), BF16)
    near_s[:, :CH, :] = tr_ref[...]
    near_g[...] = geo_ref[...].astype(BF16)

    @pl.loop(0, SLOTS)
    def _(b):
        feats[2 * NDEV + b] = source_features(geo_ref[b])

    wait_all(reqall, recv_sem.at[0])
    mine = my_index()
    copy = pltpu.make_async_copy(reqall, wanted, local_sem)
    copy.start()
    copy.wait()

    @pl.loop(0, NDEV)
    def _(a):
        for h in range(2):
            send_g[a, h] = near_g[wanted[a, h, mine]]

    send_all(lambda d: send_g.at[d], recv_g, send_sem.at[1], recv_sem.at[1])

    def gather_s():
        @pl.loop(0, NDEV)
        def _(a):
            for h in range(2):
                send_s[a, h] = near_s[wanted[a, h, mine]]

    gather_s()
    send_all(lambda d: send_s.at[d], recv_s, send_sem.at[2], recv_sem.at[2])

    def build(first, count, base):
        @pl.loop(0, SLOTS)
        def _(s):
            recv = receiver_features(geo_ref[s])
            for jj in range(first // 2, (first + count) // 2):
                pair = [feats[base + idx[s, 2 * jj + i]] for i in range(2)]
                factors[s, jj] = pair_factors(jnp.concatenate(pair, axis=0), recv)

    def applied(load, s, first, count):
        total = None
        for jj in range(first // 2, (first + count) // 2):
            lhs = jnp.concatenate([load(idx[s, 2 * jj + i]) for i in range(2)], axis=1)
            term = jnp.dot(lhs, factors[s, jj], preferred_element_type=F32)
            total = term if total is None else total + term
        return total

    def near_apply():
        @pl.loop(0, SLOTS)
        def _(s):
            acc[s] = applied(lambda i: near_s[i], s, 0, NEAR)

    def far_apply(table, out_ref, row, keep):
        r = rows_of((ROWS, V))
        mark = rows_of((8, V)) == row

        @pl.loop(0, SLOTS)
        def _(s):
            total = acc[s] + applied(lambda i: table[i // 2, i % 2], s, NEAR, FAR)
            a = alb_ref[s]
            total = total * jnp.where(r < 25, a[0:1], jnp.where(r < 50, a[1:2], a[2:3]))
            value = total.astype(BF16)
            out_ref[s] = value[:CH]
            if keep:
                near_s[s] = value
            energy = jnp.sum(total * total * geo_ref[s][6:7], axis=0, keepdims=True)
            en_all[my_index()] += jnp.where(mark, energy, 0.0)

    build(0, NEAR, 2 * NDEV)
    near_apply()
    wait_all(recv_g, recv_sem.at[1])

    @pl.loop(0, NDEV)
    def _(a):
        for h in range(2):
            feats[2 * a + h] = source_features(recv_g[a, h].astype(F32))

    build(NEAR, FAR, 0)
    wait_all(recv_s, recv_sem.at[2])
    wait_all(send_s, send_sem.at[2])
    far_apply(recv_s, b1_ref, 0, True)
    gather_s()
    send_all(lambda d: send_s.at[d], recv_s2, send_sem.at[3], recv_sem.at[3])
    near_apply()
    wait_all(recv_s2, recv_sem.at[3])
    far_apply(recv_s2, b2_ref, 1, False)
    send_all(lambda d: en_all.at[mine], en_all, send_sem.at[4], recv_sem.at[4])
    wait_all(en_all, recv_sem.at[4])
    en_ref[...] = jnp.sum(en_all[...], axis=0)
    wait_all(en_all, send_sem.at[4])
    wait_all(send_s, send_sem.at[3])
    wait_all(send_g, send_sem.at[1])
    wait_all(reqall, send_sem.at[0])


def body(transfer, positions, normals, area, albedo, pairs, home):
    vm = pl.BlockSpec(memory_space=pltpu.VMEM)
    sm = pl.BlockSpec(memory_space=pltpu.SMEM)
    idx, req = pl.pallas_call(
        index_kernel,
        out_shape=(jax.ShapeDtypeStruct((SLOTS, V), I32), jax.ShapeDtypeStruct((2, V), I32)),
        in_specs=[vm, vm],
        out_specs=(vm, vm),
    )(jnp.pad(pairs, ((0, 0), (0, V - NEAR - FAR))), home.reshape(16, V))
    geo = jnp.concatenate([positions, normals, area[:, None], jnp.ones((SLOTS, 1, V), F32)], axis=1)
    dma = pltpu.SemaphoreType.DMA
    b1, b2, en = pl.pallas_call(
        main_kernel,
        out_shape=(
            jax.ShapeDtypeStruct((SLOTS, CH, V), BF16),
            jax.ShapeDtypeStruct((SLOTS, CH, V), BF16),
            jax.ShapeDtypeStruct((8, V), F32),
        ),
        in_specs=[sm, vm, vm, vm, vm],
        out_specs=(vm, vm, vm),
        scratch_shapes=[
            pltpu.VMEM((NDEV, 2, V), I32),
            pltpu.SMEM((NDEV, 2, V), I32),
            pltpu.VMEM((NDEV, 8, V), F32),
            pltpu.VMEM((SLOTS, ROWS, V), BF16),
            pltpu.VMEM((SLOTS, 8, V), BF16),
            pltpu.VMEM((NDEV, 2, 8, V), BF16),
            pltpu.VMEM((NDEV, 2, 8, V), BF16),
            pltpu.VMEM((NDEV, 2, ROWS, V), BF16),
            pltpu.VMEM((NDEV, 2, ROWS, V), BF16),
            pltpu.VMEM((NDEV, 2, ROWS, V), BF16),
            pltpu.VMEM((2 * NDEV + SLOTS, 64, V), BF16),
            pltpu.VMEM((SLOTS, (NEAR + FAR) // 2, 2 * V, V), BF16),
            pltpu.VMEM((SLOTS, ROWS, V), F32),
            dma((5,)), dma((5,)), dma,
        ],
        compiler_params=pltpu.CompilerParams(has_side_effects=True, vmem_limit_bytes=58 * 2**20),
    )(idx, req, transfer, geo, albedo)
    energies = jnp.sum(en[:2], axis=1) * (1.0 / (NDEV * SLOTS * CH * V))
    return b1, b2, energies


def solution(mesh):
    finer = Mesh(mesh.devices.reshape(SZ), AX)
    split = [P(AX, *([None] * n)) for n in (2, 2, 2, 1, 2, 1)]
    return jax.shard_map(
        body,
        mesh=finer,
        in_specs=(*split, P()),
        out_specs=(split[0], split[0], P()),
        check_vma=False,
    )
```

profile of v0, /device:TPU:1, one launch (start us, length us, event | category | flops | bytes accessed | tf_op | source)
XLA Modules:
  0.0 195.1 jit_solution(15953827308487798548)
XLA Ops:
  0.6 0.0 copy-start.2
  0.6 0.0 copy-start.1
  0.6 0.1 pad.8.clone
  0.7 1.3 pad.4.pairs_ref
  2.1 1.7 shard_map.94
  3.8 0.0 copy-done.2
  3.8 0.8 copy.11
  4.5 1.4 maximum_maximum_fusion.geo_ref
  5.9 1.4 copy.13.alb_ref
  7.3 0.0 copy-done.1
  7.3 0.8 copy.12.tr_ref
  8.1 183.1 %shard_map.95 = (bf16[16,75,128]{2,1,0:T(8,128)(2,1)}, bf16[16,75,128]{2,1,0:T(8,128)(2,1)}, f32[8,128]{1,0:T(8,128)}) custom-call(s32[16,128]{1,0:T(8,128)} %get-tuple-element.8.idx, s32[2,128]{1,0:T(2,128)} %get-tuple-element.9.req_ref, bf16[16,75,128]{2,1,0:T(8,128)(2,1)} %copy.12.tr_ref, f32[16,8,128]{2,1,0:T(8,128)} %maximum_maximum_fusion.geo_ref, ...), custom_call_target="tpu_custom_call" | custom-call | tf_op jit(solution)/shard_map/pallas_call | solution.py:263
  191.2 0.0 copy-start
  191.2 1.8 copy.14
  193.0 0.8 slice_reduce_fusion
  193.8 0.5 broadcast_multiply_fusion
  194.3 0.0 copy-done
  194.3 0.8 copy.15
  (1 shorter events, 0.0 us)
Async XLA Ops:
  0.6 3.1 %copy-start.2 = (f32[16,3,128]{2,0,1:T(8,128)S(1)}, f32[16,3,128]{2,0,1:T(8,128)}, u32[]{:S(2)}) copy-start(f32[16,3,128]{2,0,1:T(8,128)} %param.8) | copy-start | bytes 73732
  0.6 6.7 %copy-start.1 = (bf16[16,75,128]{2,0,1:T(8,128)(2,1)S(1)}, bf16[16,75,128]{2,0,1:T(8,128)(2,1)}, u32[]{:S(2)}) copy-start(bf16[16,75,128]{2,0,1:T(8,128)(2,1)} %param.7) | copy-start | bytes 921604
  191.2 3.1 %copy-start = (bf16[16,75,128]{2,1,0:T(8,128)(2,1)S(1)}, bf16[16,75,128]{2,1,0:T(8,128)(2,1)}, u32[]{:S(2)}) copy-start(bf16[16,75,128]{2,1,0:T(8,128)(2,1)} %get-tuple-element.14) | copy-start | bytes 921604
where the time goes:
time: 195 us
  Pallas kernels  185 us (95%)
  local copies, waits for them, and re-layouts  6.96 us (4%)
  other arithmetic  2.7 us (1%)
    pallas_call x1, Pallas kernels, body(): pl.pallas_call(main_kernel, out_shape=(jax.ShapeDtypeStruct((SLOTS, CH, V...  183 us
    unnamed x12, local copies, waits for them, and re-layouts  5.56 us

commit v1 on v0

--- a/solution.py
+++ b/solution.py
@@ -132,58 +132,198 @@
 OFFSETS = [o for o in itertools.product(range(4), range(2), range(4), range(4)) if any(o)]
 ORDER = [OFFSETS[i] for i in np.random.RandomState(0).permutation(len(OFFSETS))]
 
-
-def send_all(src_of, dst, send_sem, recv_sem):
-    mine = my_index()
-    for off in ORDER:
-        to = shifted(off)
-        pltpu.make_async_remote_copy(
-            src_of(flat(to)), dst.at[mine], send_sem, recv_sem, device_id=to, device_id_type=MESH
-        ).start()
-
-
-def wait_all(buf, sem):
-    part = buf.at[pl.ds(0, NDEV - 1)]
+DIMS = (0, 2, 3)
+PLANES = ((2, 3), (0, 3), (0, 2))
+SEG = 24
+GEO = ((0, 1, 2), (3, 4), (5, 6))
+
+
+def hops(off):
+    return sum(min(off[d], 4 - off[d]) for d in DIMS)
+
+
+def moved(dim, by):
+    off = [0, 0, 0, 0]
+    off[dim] = by
+    return tuple(off)
+
+
+def plane_offsets(k):
+    a, b = PLANES[k]
+    out = []
+    for i, j, c in itertools.product(range(4), range(4), range(2)):
+        off = [0, c, 0, 0]
+        off[a], off[b] = i, j
+        if any(off):
+            out.append(tuple(off))
+    order = np.random.RandomState(k).permutation(len(out))
+    return sorted((out[i] for i in order), key=lambda o: -hops(o))
+
+
+def plane_index(k, t):
+    a, b = PLANES[k]
+    return (t[b] * 4 + t[a]) * 2 + t[1]
+
+
+def send(src, dst, send_sem, recv_sem, to):
+    pltpu.make_async_remote_copy(
+        src, dst, send_sem, recv_sem, device_id=to, device_id_type=MESH
+    ).start()
+
+
+def wait_for(part, sem):
     pltpu.make_async_copy(part, part, sem).wait()
+
+
+def row_column(shape):
+    return rows_of(shape), lax.broadcasted_iota(I32, shape, 1)
+
+
+def selection(k, table):
+    r, m = row_column((256, 64))
+    expand = jnp.where(m == ((r >> 3) << 1) + (r & 1), 1.0, 0.0).astype(BF16)
+    wide = jnp.dot(expand, table.astype(F32).astype(BF16), preferred_element_type=F32)
+    r, lane = row_column((256, V))
+    coords = list(me4())
+    coords[DIMS[k]] = (r >> 1) & 3
+    value = jnp.sum(jnp.where(lane == flat(coords), wide, 0.0), axis=1, keepdims=True)
+    place = (lane - (((r >> 1) & 3) << 4)).astype(F32)
+    return jnp.where(value == place, 1.0, 0.0)[:, :64].astype(BF16)
+
+
+def canonical(k):
+    r, col = row_column((256, 256))
+    t = (r >> 6, (r >> 5) & 1, (r >> 3) & 3, (r >> 1) & 3)
+    place = (plane_index(k, t) << 3) + (t[DIMS[k]] << 1) + (r & 1)
+    return jnp.where(place == col, 1.0, 0.0).astype(BF16)
 
 
 def main_kernel(
     idx, req_ref, tr_ref, geo_ref, alb_ref, b1_ref, b2_ref, en_ref,
-    reqall, wanted, en_all, near_s, near_g, send_g, recv_g, send_s, recv_s, recv_s2,
-    feats, factors, acc, send_sem, recv_sem, local_sem,
+    r0, r1, r2, wanted, near_s, la0, la1, la2, lb0, lb1, lb2, lc0, lc1, lc2, lr, sel,
+    sg0, sg1, sg2, rg0, rg1, rg2, sr, rr, ss, tab_a, tab_b, geo_t, rem_t, tail,
+    feats, factors, acc, en_all, sem_r, sem_rs, sem_b, sem_bs, sem_c, sem_cs, sem_u, sem_us,
+    sem_g, sem_gs, sem_e, local_sem,
 ):
-    send_all(lambda d: req_ref, reqall, send_sem.at[0], recv_sem.at[0])
-    reqall[my_index()] = req_ref[...]
-    en_all[my_index()] = jnp.zeros((8, V), F32)
+    lc, sg, rg = (lc0, lc1, lc2), (sg0, sg1, sg2), (rg0, rg1, rg2)
+    line_a, line_b = (la0, la1, la2), (lb0, lb1, lb2)
+    here = me4()
+    core = here[1]
+    pos = [here[d] for d in DIMS]
+    partner = shifted((0, 1, 0, 0))
+    lines = [[shifted(moved(d, by)) for by in (2, 1, 3)] for d in DIMS]
+
+    barrier = pltpu.get_barrier_semaphore()
+    for to in [partner] + sum(lines, []):
+        pl.semaphore_signal(barrier, inc=1, device_id=to, device_id_type=MESH)
     near_s[:, 64:, :] = jnp.zeros((SLOTS, ROWS - 64, V), BF16)
     near_s[:, :CH, :] = tr_ref[...]
-    near_g[...] = geo_ref[...].astype(BF16)
+    r0[core] = req_ref[...]
+
+    def fill_lines(line):
+        for k in range(3):
+            line[k][pos[k]] = near_s[:, SEG * k : SEG * (k + 1), :]
+
+    def rem_rows(k):
+        rows = near_s[:, 72:80, :].astype(F32)
+        return rows[:, k, :].astype(BF16)
+
+    fill_lines(line_a)
+    for k in range(3):
+        lc[k][pos[k], 0] = rem_rows(k)
+        for g, comp in enumerate(GEO[k]):
+            lc[k][pos[k], 1 + g] = geo_ref[:, comp, :].astype(BF16)
+    pl.semaphore_wait(barrier, 10)
+
+    send(req_ref, r0.at[core], sem_rs.at[0], sem_r.at[0], partner)
+
+    def send_lines(line, n):
+        for by in range(3):
+            for k in range(3):
+                part = line[k].at[pos[k]]
+                send(part, part, sem_bs.at[n, k], sem_b.at[n, k], lines[k][by])
+
+    for by in range(3):
+        for k in range(3):
+            part = lc[k].at[pos[k]]
+            send(part, part, sem_cs.at[0, k], sem_c.at[0, k], lines[k][by])
+    wait_for(r0.at[0], sem_r.at[0])
+    for i in range(3):
+        r1[i, pl.ds(pos[i] * 2, 2)] = r0[...]
+        for to in lines[i]:
+            send(r0, r1.at[i, pl.ds(pos[i] * 2, 2)], sem_rs.at[1 + i], sem_r.at[1 + i], to)
+    send_lines(line_a, 0)
+    for i in range(3):
+        wait_for(r1.at[i, pl.ds(0, 6)], sem_r.at[1 + i])
+    for k in range(3):
+        ia, ib = (DIMS.index(d) for d in PLANES[k])
+        part = r2.at[k, pl.ds(pos[ib] * 8, 8)]
+        r2[k, pl.ds(pos[ib] * 8, 8)] = r1[ia]
+        for to in lines[ib]:
+            send(r1.at[ia], part, sem_rs.at[4 + k], sem_r.at[4 + k], to)
+
+    rem_t[...] = jnp.zeros((2 * NDEV, 8, V), F32)
+    geo_t[:, 7, :] = jnp.ones((2 * NDEV, V), F32)
+    en_all[my_index()] = jnp.zeros((2, V), F32)
 
     @pl.loop(0, SLOTS)
     def _(b):
         feats[2 * NDEV + b] = source_features(geo_ref[b])
 
-    wait_all(reqall, recv_sem.at[0])
-    mine = my_index()
-    copy = pltpu.make_async_copy(reqall, wanted, local_sem)
+    for k in range(3):
+        wait_for(r2.at[k, pl.ds(0, 24)], sem_r.at[4 + k])
+    copy = pltpu.make_async_copy(r2, wanted, local_sem)
     copy.start()
+    for k in range(3):
+        table = jnp.concatenate([r2[k, i] for i in range(32)], axis=0)
+        sel[k] = selection(k, table)
     copy.wait()
 
-    @pl.loop(0, NDEV)
-    def _(a):
-        for h in range(2):
-            send_g[a, h] = near_g[wanted[a, h, mine]]
-
-    send_all(lambda d: send_g.at[d], recv_g, send_sem.at[1], recv_sem.at[1])
-
-    def gather_s():
-        @pl.loop(0, NDEV)
-        def _(a):
-            for h in range(2):
-                send_s[a, h] = near_s[wanted[a, h, mine]]
-
-    gather_s()
-    send_all(lambda d: send_s.at[d], recv_s, send_sem.at[2], recv_sem.at[2])
+    for k in range(3):
+        wait_for(lc[k].at[pl.ds(0, 3)], sem_c.at[0, k])
+        for g in range(1 + len(GEO[k])):
+            source = lc[k][:, g].reshape(64, V)
+            got = jnp.dot(sel[k], source, preferred_element_type=F32).astype(BF16)
+            sg[k][:, g] = got.reshape(32, 8, V)
+        mine = plane_index(k, here)
+        rg[k][mine] = sg[k][mine]
+        for off in plane_offsets(k):
+            to = shifted(off)
+            send(sg[k].at[plane_index(k, to)], rg[k].at[mine], sem_gs.at[0, k], sem_g.at[0, k], to)
+
+    def owner_slice(ref, k, t):
+        at = [t[0], t[1], t[2], t[3]]
+        at[DIMS[k]] = slice(None)
+        return ref.at[at[0], at[1], at[2], at[3], :, pl.ds(SEG * k, SEG), :]
+
+    def spread(line, tab, n):
+        for k in range(3):
+            wait_for(line[k].at[pl.ds(0, 3)], sem_b.at[n, k])
+            owners = []
+            for o in range(4):
+                t = list(here)
+                t[DIMS[k]] = o
+                owners.append(t)
+            flat_owner = [flat(t) for t in owners]
+
+            @pl.loop(0, 32)
+            def _(d):
+                for o in range(4):
+                    for h in range(2):
+                        ss[k, d, o, h] = line[k][o, wanted[k, d, h, flat_owner[o]]]
+
+            mine = plane_index(k, here)
+            for o in range(4):
+                t = owners[o]
+                for h in range(2):
+                    block = line[k][o, wanted[k, mine, h, flat_owner[o]]]
+                    tab[t[0], t[1], t[2], t[3], h, SEG * k : SEG * (k + 1), :] = block
+            for off in plane_offsets(k):
+                to = shifted(off)
+                send(ss.at[k, plane_index(k, to)], owner_slice(tab, k, here),
+                     sem_us.at[n, k], sem_u.at[n, k], to)
+
+    spread(line_a, tab_a, 0)
 
     def build(first, count, base):
         @pl.loop(0, SLOTS)
@@ -206,47 +346,94 @@
         def _(s):
             acc[s] = applied(lambda i: near_s[i], s, 0, NEAR)
 
-    def far_apply(table, out_ref, row, keep):
+    def far_apply(tab, out_ref, row):
         r = rows_of((ROWS, V))
-        mark = rows_of((8, V)) == row
+        mark = rows_of((2, V)) == row
+
+        def load(i):
+            head = tab[i >> 6, (i >> 5) & 1, (i >> 3) & 3, (i >> 1) & 3, i & 1]
+            return jnp.concatenate([head, tail[i]], axis=0)
 
         @pl.loop(0, SLOTS)
         def _(s):
-            total = acc[s] + applied(lambda i: table[i // 2, i % 2], s, NEAR, FAR)
+            total = acc[s] + applied(load, s, NEAR, FAR)
             a = alb_ref[s]
             total = total * jnp.where(r < 25, a[0:1], jnp.where(r < 50, a[1:2], a[2:3]))
             value = total.astype(BF16)
             out_ref[s] = value[:CH]
-            if keep:
+            if row == 0:
                 near_s[s] = value
             energy = jnp.sum(total * total * geo_ref[s][6:7], axis=0, keepdims=True)
             en_all[my_index()] += jnp.where(mark, energy, 0.0)
 
+    def tails(rows_of_part):
+        for k in range(3):
+            rem_t[:, k, :] = jnp.dot(canonical(k), rows_of_part(k), preferred_element_type=F32)
+        tail[...] = rem_t[...].astype(BF16)
+
     build(0, NEAR, 2 * NDEV)
     near_apply()
-    wait_all(recv_g, recv_sem.at[1])
-
-    @pl.loop(0, NDEV)
-    def _(a):
-        for h in range(2):
-            feats[2 * a + h] = source_features(recv_g[a, h].astype(F32))
+    for k in range(3):
+        wait_for(rg[k].at[pl.ds(0, 31)], sem_g.at[0, k])
+        order = canonical(k)
+        for g, comp in enumerate(GEO[k]):
+            rows = rg[k][:, 1 + g].reshape(256, V)
+            geo_t[:, comp, :] = jnp.dot(order, rows, preferred_element_type=F32)
+    tails(lambda k: rg[k][:, 0].reshape(256, V))
+
+    @pl.loop(0, 2 * NDEV)
+    def _(b):
+        feats[b] = source_features(geo_t[b])
 
     build(NEAR, FAR, 0)
-    wait_all(recv_s, recv_sem.at[2])
-    wait_all(send_s, send_sem.at[2])
-    far_apply(recv_s, b1_ref, 0, True)
-    gather_s()
-    send_all(lambda d: send_s.at[d], recv_s2, send_sem.at[3], recv_sem.at[3])
+    for k in range(3):
+        wait_for(ss.at[k, pl.ds(0, 31)], sem_u.at[0, k])
+    far_apply(tab_a, b1_ref, 0)
+
+    fill_lines(line_b)
+    for k in range(3):
+        lr[k, pos[k]] = rem_rows(k)
+    for by in range(3):
+        for k in range(3):
+            part = lr.at[k, pos[k]]
+            send(part, part, sem_cs.at[1, k], sem_c.at[1, k], lines[k][by])
+    send_lines(line_b, 1)
     near_apply()
-    wait_all(recv_s2, recv_sem.at[3])
-    far_apply(recv_s2, b2_ref, 1, False)
-    send_all(lambda d: en_all.at[mine], en_all, send_sem.at[4], recv_sem.at[4])
-    wait_all(en_all, recv_sem.at[4])
+    for k in range(3):
+        wait_for(ss.at[k, pl.ds(0, 31)], sem_us.at[0, k])
+        wait_for(lr.at[k, pl.ds(0, 3)], sem_c.at[1, k])
+        got = jnp.dot(sel[k], lr[k].reshape(64, V), preferred_element_type=F32).astype(BF16)
+        sr[k] = got.reshape(32, 8, V)
+        mine = plane_index(k, here)
+        rr[k, mine] = sr[k, mine]
+        for off in plane_offsets(k):
+            to = shifted(off)
+            send(sr.at[k, plane_index(k, to)], rr.at[k, mine], sem_gs.at[1, k], sem_g.at[1, k], to)
+    spread(line_b, tab_b, 1)
+    for k in range(3):
+        wait_for(rr.at[k, pl.ds(0, 31)], sem_g.at[1, k])
+    tails(lambda k: rr[k].reshape(256, V))
+    for k in range(3):
+        wait_for(ss.at[k, pl.ds(0, 31)], sem_u.at[1, k])
+    far_apply(tab_b, b2_ref, 1)
+
+    mine = my_index()
+    for off in ORDER:
+        send(en_all.at[mine], en_all.at[mine], sem_e.at[0], sem_e.at[1], shifted(off))
+    wait_for(en_all.at[pl.ds(0, NDEV - 1)], sem_e.at[1])
     en_ref[...] = jnp.sum(en_all[...], axis=0)
-    wait_all(en_all, send_sem.at[4])
-    wait_all(send_s, send_sem.at[3])
-    wait_all(send_g, send_sem.at[1])
-    wait_all(reqall, send_sem.at[0])
+    wait_for(en_all.at[pl.ds(0, NDEV - 1)], sem_e.at[0])
+    wait_for(r0.at[0], sem_rs.at[0])
+    for i in range(3):
+        wait_for(r1.at[i, pl.ds(0, 6)], sem_rs.at[1 + i])
+        wait_for(r2.at[i, pl.ds(0, 24)], sem_rs.at[4 + i])
+        wait_for(lc[i].at[pl.ds(0, 3)], sem_cs.at[0, i])
+        wait_for(lr.at[i, pl.ds(0, 3)], sem_cs.at[1, i])
+        wait_for(rg[i].at[pl.ds(0, 31)], sem_gs.at[0, i])
+        wait_for(rr.at[i, pl.ds(0, 31)], sem_gs.at[1, i])
+        wait_for(ss.at[i, pl.ds(0, 31)], sem_us.at[1, i])
+        for n, line in enumerate((line_a, line_b)):
+            wait_for(line[i].at[pl.ds(0, 3)], sem_bs.at[n, i])
 
 
 def body(transfer, positions, normals, area, albedo, pairs, home):
@@ -265,29 +452,40 @@
         out_shape=(
             jax.ShapeDtypeStruct((SLOTS, CH, V), BF16),
             jax.ShapeDtypeStruct((SLOTS, CH, V), BF16),
-            jax.ShapeDtypeStruct((8, V), F32),
+            jax.ShapeDtypeStruct((2, V), F32),
         ),
         in_specs=[sm, vm, vm, vm, vm],
         out_specs=(vm, vm, vm),
         scratch_shapes=[
-            pltpu.VMEM((NDEV, 2, V), I32),
-            pltpu.SMEM((NDEV, 2, V), I32),
-            pltpu.VMEM((NDEV, 8, V), F32),
+            pltpu.VMEM((2, 2, V), I32),
+            pltpu.VMEM((3, 8, 2, V), I32),
+            pltpu.VMEM((3, 32, 2, V), I32),
+            pltpu.SMEM((3, 32, 2, V), I32),
             pltpu.VMEM((SLOTS, ROWS, V), BF16),
-            pltpu.VMEM((SLOTS, 8, V), BF16),
-            pltpu.VMEM((NDEV, 2, 8, V), BF16),
-            pltpu.VMEM((NDEV, 2, 8, V), BF16),
-            pltpu.VMEM((NDEV, 2, ROWS, V), BF16),
-            pltpu.VMEM((NDEV, 2, ROWS, V), BF16),
-            pltpu.VMEM((NDEV, 2, ROWS, V), BF16),
+            *[pltpu.VMEM((4, SLOTS, SEG, V), BF16) for _ in range(6)],
+            *[pltpu.VMEM((4, 1 + len(g), SLOTS, V), BF16) for g in GEO],
+            pltpu.VMEM((3, 4, SLOTS, V), BF16),
+            pltpu.VMEM((3, 256, 64), BF16),
+            *[pltpu.VMEM((32, 1 + len(g), 8, V), BF16) for g in GEO],
+            *[pltpu.VMEM((32, 1 + len(g), 8, V), BF16) for g in GEO],
+            pltpu.VMEM((3, 32, 8, V), BF16),
+            pltpu.VMEM((3, 32, 8, V), BF16),
+            pltpu.VMEM((3, 32, 4, 2, SEG, V), BF16),
+            pltpu.VMEM((4, 2, 4, 4, 2, 3 * SEG, V), BF16),
+            pltpu.VMEM((4, 2, 4, 4, 2, 3 * SEG, V), BF16),
+            pltpu.VMEM((2 * NDEV, 8, V), F32),
+            pltpu.VMEM((2 * NDEV, 8, V), F32),
+            pltpu.VMEM((2 * NDEV, 8, V), BF16),
             pltpu.VMEM((2 * NDEV + SLOTS, 64, V), BF16),
             pltpu.VMEM((SLOTS, (NEAR + FAR) // 2, 2 * V, V), BF16),
             pltpu.VMEM((SLOTS, ROWS, V), F32),
-            dma((5,)), dma((5,)), dma,
+            pltpu.VMEM((NDEV, 2, V), F32),
+            dma((7,)), dma((7,)), dma((2, 3)), dma((2, 3)), dma((2, 3)), dma((2, 3)),
+            dma((2, 3)), dma((2, 3)), dma((2, 3)), dma((2, 3)), dma((2,)), dma,
         ],
-        compiler_params=pltpu.CompilerParams(has_side_effects=True, vmem_limit_bytes=58 * 2**20),
+        compiler_params=pltpu.CompilerParams(collective_id=0, has_side_effects=True, vmem_limit_bytes=58 * 2**20),
     )(idx, req, transfer, geo, albedo)
-    energies = jnp.sum(en[:2], axis=1) * (1.0 / (NDEV * SLOTS * CH * V))
+    energies = jnp.sum(en, axis=1) * (1.0 / (NDEV * SLOTS * CH * V))
     return b1, b2, energies
 
 

time: 195 us -> 158 us (0.81)
  Pallas kernels: 185 us -> 148 us
    pallas_call x1, Pallas kernels: 183 us -> 146 us  [body(): pl.pallas_call(main_kernel, out_shape=(jax.ShapeDtypeStruct((SLOTS, CH, V...]
    unnamed x12 -> x14, local copies, waits for them, and re-layouts: 5.56 us -> 5.56 us
where the time goes in v1:
time: 158 us
  Pallas kernels  148 us (94%)
  local copies, waits for them, and re-layouts  6.97 us (4%)
  other arithmetic  2.03 us (1%)
    pallas_call x1, Pallas kernels, body(): pl.pallas_call(main_kernel, out_shape=(jax.ShapeDtypeStruct((SLOTS, CH, V...  146 us
    unnamed x14, local copies, waits for them, and re-layouts  5.56 us

profile of v1, /device:TPU:1, one launch (start us, length us, event | category | flops | bytes accessed | tf_op | source)
XLA Modules:
  0.0 157.8 jit_solution(13985294340153909709)
XLA Ops:
  0.6 0.0 copy-start.2
  0.6 0.0 copy-start.1
  0.6 0.1 pad.8.clone
  0.7 1.3 pad.4.pairs_ref
  2.1 1.7 %shard_map.94 = (s32[16,128]{1,0:T(8,128)}, s32[2,128]{1,0:T(2,128)}) custom-call(s32[16,128]{1,0:T(8,128)} %pad.4.pairs_ref, s32[16,128]{1,0:T(8,128)} %bitcast.4), custom_call_target="tpu_custom_call" | custom-call | tf_op jit(solution)/shard_map/pallas_call | solution.py:442
  3.8 0.0 copy-done.2
  3.8 0.8 copy.11
  4.5 1.4 maximum_maximum_fusion.geo_ref
  5.9 1.4 copy.13.alb_ref
  7.3 0.0 copy-done.1
  7.3 0.8 copy.12.tr_ref
  8.1 146.5 %shard_map.95 = (bf16[16,75,128]{2,1,0:T(8,128)(2,1)}, bf16[16,75,128]{2,1,0:T(8,128)(2,1)}, f32[2,128]{1,0:T(2,128)}) custom-call(s32[16,128]{1,0:T(8,128)} %get-tuple-element.8.idx, s32[2,128]{1,0:T(2,128)} %get-tuple-element.9.req_ref, bf16[16,75,128]{2,1,0:T(8,128)(2,1)} %copy.12.tr_ref, f32[16,8,128]{2,1,0:T(8,128)} %maximum_maximum_fusion.geo_ref, ...), custom_call_target="tpu_custom_call" | custom-call | tf_op jit(solution)/shard_map/pallas_call | solution.py:450
  154.6 0.0 copy-start
  154.6 0.0 copy-start.3
  154.6 1.8 %copy.14 = bf16[16,75,128]{2,0,1:T(8,128)(2,1)} copy(bf16[16,75,128]{2,1,0:T(8,128)(2,1)} %get-tuple-element.13) | data formatting | bytes 614400
  156.4 0.0 copy-done.3
  156.4 0.1 reduce_sum.9
  156.5 0.5 broadcast_multiply_fusion
  157.0 0.0 copy-done
  157.0 0.8 copy.15
  (1 shorter events, 0.0 us)
Async XLA Ops:
  0.6 3.1 %copy-start.2 = (f32[16,3,128]{2,0,1:T(8,128)S(1)}, f32[16,3,128]{2,0,1:T(8,128)}, u32[]{:S(2)}) copy-start(f32[16,3,128]{2,0,1:T(8,128)} %param.8) | copy-start | bytes 73732
  0.6 6.7 %copy-start.1 = (bf16[16,75,128]{2,0,1:T(8,128)(2,1)S(1)}, bf16[16,75,128]{2,0,1:T(8,128)(2,1)}, u32[]{:S(2)}) copy-start(bf16[16,75,128]{2,0,1:T(8,128)(2,1)} %param.7) | copy-start | bytes 921604
  154.6 2.5 %copy-start = (bf16[16,75,128]{2,1,0:T(8,128)(2,1)S(1)}, bf16[16,75,128]{2,1,0:T(8,128)(2,1)}, u32[]{:S(2)}) copy-start(bf16[16,75,128]{2,1,0:T(8,128)(2,1)} %get-tuple-element.14) | copy-start | bytes 921604
  154.6 1.8 %copy-start.3 = (f32[2,128]{1,0:T(2,128)S(1)}, f32[2,128]{1,0:T(2,128)}, u32[]{:S(2)}) copy-start(f32[2,128]{1,0:T(2,128)} %get-tuple-element.12) | copy-start | bytes 3076

commit v2 on v0

v2 whole, which is shorter than its diff:
```python
import itertools
import types

import jax
import jax.numpy as jnp
import numpy as np
from jax import lax
from jax.experimental import pallas as pl
from jax.experimental.pallas import tpu as pltpu
from jax.sharding import Mesh
from jax.sharding import PartitionSpec as P

AX = ("y", "c", "z", "x")
SZ = (4, 2, 4, 4)
NDEV = 128
SLOTS, NEAR, FAR, CH, V = 16, 16, 24, 75, 128
ROWS = 80
F32, BF16, I32 = jnp.float32, jnp.bfloat16, jnp.int32
MESH = pl.DeviceIdType.MESH


def rounded(t):
    return t.astype(BF16).astype(F32)


def pieces3(t):
    a = rounded(t)
    b = rounded(t - a)
    return a, b, rounded(t - a - b)


def rows_of(shape):
    return lax.broadcasted_iota(I32, shape, 0)


def source_features(v):
    r = rows_of((8, V))
    vh = rounded(v)
    vl = rounded(v - vh)
    m = -(v * v[6:7])
    mh = rounded(m)
    ml = rounded(m - mh)
    x = jnp.where(r < 3, v, 0.0)
    c = pieces3(jnp.sum(pltpu.roll(m, 5, 0) * x, axis=0, keepdims=True))
    e = pieces3(jnp.sum(x * x, axis=0, keepdims=True) + 1.0)
    cv = jnp.ones((8, V), F32)
    for i, row in enumerate(c + e):
        cv = jnp.where(r == i, row, cv)
    return jnp.concatenate([vh, vh, vl, mh, mh, ml, cv, jnp.zeros((8, V), F32)], axis=0).astype(BF16)


def receiver_features(v):
    r = rows_of((8, V))
    z = jnp.zeros((8, V), F32)
    x = jnp.where(r < 3, v, 0.0)
    n = jnp.where(r < 3, pltpu.roll(v, 5, 0), 0.0) * (1.0 / np.pi)
    nh = rounded(n)
    nl = rounded(n - nh)
    xh = rounded(x)
    xl = rounded(x - xh)
    k = pieces3(-jnp.sum(n * x, axis=0, keepdims=True))
    q = pieces3(jnp.sum(x * x, axis=0, keepdims=True))
    xh3 = -pltpu.roll(xh, 3, 0)
    xl3 = -pltpu.roll(xl, 3, 0)
    last = r == 7
    ap = [jnp.where(last, k[0], nh), jnp.where(last, k[1], nl), nh, z, z, z, jnp.where(r == 6, k[2], z), z]
    aq = [z, z, z, xh3, xl3, xh3, jnp.where(r < 3, 1.0, z), z]
    d = [jnp.where(last, q[0], -2.0 * xh), jnp.where(last, q[1], -2.0 * xl), -2.0 * xh, z, z, z,
         jnp.where((r >= 3) & (r < 6), 1.0, jnp.where(r == 6, q[2], z)), z]
    ap, aq, d = (jnp.concatenate(t, axis=0).astype(BF16) for t in (ap, aq, d))
    o = jnp.zeros((64, V), BF16)
    top = jnp.concatenate([ap, aq, o, o, d, o], axis=1)
    bottom = jnp.concatenate([o, o, ap, aq, o, d], axis=1)
    return jnp.concatenate([top, bottom], axis=0)


def pair_factors(feats, recv):
    out = lax.dot_general(feats, recv, (((0,), (0,)), ((), ())), preferred_element_type=F32)
    parts = []
    for i in range(2):
        ap = out[:, 256 * i : 256 * i + 128]
        aq = out[:, 256 * i + 128 : 256 * i + 256]
        d = out[:, 512 + 128 * i : 640 + 128 * i]
        parts.append((jnp.maximum(ap, 0.0) * jnp.maximum(aq, 0.0) / (d * d)).astype(BF16))
    return jnp.concatenate(parts, axis=0)


def me4():
    return tuple(lax.axis_index(a) for a in AX)


def my_index():
    y, c, z, x = me4()
    return ((y * 2 + c) * 4 + z) * 4 + x


def shifted(off):
    return tuple(lax.rem(i + o, s) for i, o, s in zip(me4(), off, SZ))


def flat(t):
    return ((t[0] * 2 + t[1]) * 4 + t[2]) * 4 + t[3]


def index_kernel(pairs_ref, home_ref, idx_ref, req_ref, wide_ref):
    wide_ref[...] = jnp.zeros((SLOTS, V), I32)
    wide_ref[:, : NEAR + FAR] = pairs_ref[...]
    p = wide_ref[...]
    home = home_ref[...]
    shape = (SLOTS, V)
    lane = lax.broadcasted_iota(I32, shape, 1)
    low, high = p & 127, p >> 7
    slot = jnp.zeros(shape, I32)
    for h in range(16):
        got = jnp.take_along_axis(jnp.broadcast_to(home[h : h + 1], shape), low, axis=1)
        slot = jnp.where(high == h, got, slot)
    owner, local = slot >> 4, slot & 15
    lo = jnp.full(shape, 99, I32)
    hi = jnp.full(shape, -1, I32)
    for j in range(NEAR, NEAR + FAR):
        same = owner[:, j : j + 1] == lane
        lo = jnp.where(same, jnp.minimum(lo, local[:, j : j + 1]), lo)
        hi = jnp.where(same, jnp.maximum(hi, local[:, j : j + 1]), hi)
    lo = jnp.min(lo, axis=0, keepdims=True)
    hi = jnp.max(hi, axis=0, keepdims=True)
    lo = jnp.where(lo > 15, 0, lo)
    hi = jnp.where(hi < 0, 0, hi)
    first = jnp.take_along_axis(jnp.broadcast_to(lo, shape), owner, axis=1)
    far = owner * 2 + jnp.where(local != first, 1, 0)
    idx_ref[...] = jnp.where(lane < NEAR, local, far)
    req_ref[...] = jnp.where(rows_of((2, V)) == 0, lo, hi)


OFFSETS = [o for o in itertools.product(range(4), range(2), range(4), range(4)) if any(o)]
ORDER = [OFFSETS[i] for i in np.random.RandomState(0).permutation(len(OFFSETS))]

DIMS = (0, 2, 3)
AXES = ((0, 2, 3), (2, 3, 0), (3, 0, 2))
STEPS = (2, 1, 3)
SEG = 24
GEO = ((0, 1, 2), (3, 4), (5, 6))
FROM = (0, 3, 2, 1)


def moved(dim, by, core=0):
    off = [0, core, 0, 0]
    off[dim] = by
    return tuple(off)


def send(src, dst, send_sem, recv_sem, to):
    pltpu.make_async_remote_copy(
        src, dst, send_sem, recv_sem, device_id=to, device_id_type=MESH
    ).start()


def wait_for(part, sem):
    pltpu.make_async_copy(part, part, sem).wait()


def row_column(shape):
    return rows_of(shape), lax.broadcasted_iota(I32, shape, 1)


def selection(k, table):
    here = me4()
    a, b, _ = AXES[k]
    r, m = row_column((256, 16))
    expand = jnp.where(m == ((r >> 5) << 1) + (r & 1), 1.0, 0.0).astype(BF16)
    wide = jnp.dot(expand, table.astype(F32).astype(BF16), preferred_element_type=F32)
    r, lane = row_column((256, V))
    coords = list(here)
    coords[a] = (here[a] + ((r >> 1) & 3)) & 3
    coords[b] = (here[b] + ((r >> 3) & 3)) & 3
    value = jnp.sum(jnp.where(lane == flat(coords), wide, 0.0), axis=1, keepdims=True)
    r, lane = row_column((256, 256))
    place = (lane - (((r >> 1) & 15) << 4)).astype(F32)
    return jnp.where(value == place, 1.0, 0.0).astype(BF16)


def canonical(k):
    here = me4()
    a, b, c = AXES[k]
    r, col = row_column((256, 256))
    t = (r >> 6, (r >> 5) & 1, (r >> 3) & 3, (r >> 1) & 3)
    i = (t[a] - here[a]) & 3
    j = (t[b] - here[b]) & 3
    place = (((t[c] << 1) + t[1]) << 5) + (j << 3) + (i << 1) + (r & 1)
    return jnp.where(place == col, 1.0, 0.0).astype(BF16)


def main_kernel(idx, req_ref, tr_ref, pos_ref, nrm_ref, area_ref, alb_ref, b1_ref, b2_ref, en_ref, *scratch):
    w = types.SimpleNamespace(**dict(zip([n for n, _ in scratch_list()], scratch)))
    factors, feats, acc, near_s = w.factors, w.feats, w.acc, w.near_s
    cp, sg, rg = (w.cp0, w.cp1, w.cp2), (w.sg0, w.sg1, w.sg2), (w.rg0, w.rg1, w.rg2)
    planes = [[[getattr(w, f"p{n}{k}{j}") for j in range(4)] for k in range(3)] for n in range(2)]
    tabs = (w.tab_a, w.tab_b)
    here = me4()
    core = here[1]
    mine = my_index()
    partner = shifted((0, 1, 0, 0))
    line = {d: {by: shifted(moved(d, by)) for by in STEPS} for d in DIMS}
    other = {d: {by: shifted(moved(d, by, 1)) for by in STEPS} for d in DIMS}

    barrier = pltpu.get_barrier_semaphore()
    greeted = [partner] + [t[d][by] for t in (line, other) for d in DIMS for by in STEPS]
    for to in greeted:
        pl.semaphore_signal(barrier, inc=1, device_id=to, device_id_type=MESH)

    for i in range(3):
        w.r1[i, here[DIMS[i]] * 2 + core] = req_ref[...]
    w.wide[:CH] = tr_ref[...].astype(F32)
    w.wide[CH:] = jnp.zeros((ROWS - CH, SLOTS, V), F32)
    comps = [pos_ref.at[0], pos_ref.at[1], pos_ref.at[2], nrm_ref.at[0], nrm_ref.at[1], nrm_ref.at[2], area_ref]
    for i, comp in enumerate(comps):
        w.geo[:, i, :] = comp[...]
    w.geo[:, 7, :] = jnp.ones((SLOTS, V), F32)
    for s in range(SLOTS):
        value = w.wide[:, s, :].astype(BF16)
        near_s[s] = value
        for k in range(3):
            planes[0][k][0][0, s] = value[SEG * k : SEG * (k + 1)]
    for k in range(3):
        cp[k][0, 0, 0] = tr_ref[72 + k]
        for g, comp in enumerate(GEO[k]):
            cp[k][0, 0, 1 + g] = comps[comp][...].astype(BF16)
    pl.semaphore_wait(barrier, len(greeted))

    for i in range(3):
        slot = w.r1.at[i, here[DIMS[i]] * 2 + core]
        for to in [line[DIMS[i]][by] for by in STEPS] + [other[DIMS[i]][by] for by in STEPS] + [partner]:
            send(req_ref, slot, w.sem_rs.at[i], w.sem_r.at[i], to)

    def first_leg(refs, send_sem, recv_sem):
        for by in STEPS:
            for k in range(3):
                send(refs[k].at[0], refs[k].at[FROM[by]], send_sem.at[k], recv_sem.at[k], line[AXES[k][0]][by])

    first_leg([c.at[0] for c in cp], w.sem_c1s, w.sem_c1)
    first_leg([p[0] for p in planes[0]], w.sem_b1s.at[0], w.sem_b1.at[0])

    def second_leg(n, part, size):
        for by in STEPS:
            for k in range(3):
                send(planes[n][k][0].at[pl.ds(part, size)], planes[n][k][FROM[by]].at[pl.ds(part, size)],
                     w.sem_b2s.at[n, k], w.sem_b2.at[n, k, FROM[by]], line[AXES[k][1]][by])

    def lines_second_leg(refs, send_sem, recv_sem):
        for by in STEPS:
            for k in range(3):
                send(refs[k].at[0], refs[k].at[FROM[by]], send_sem.at[k], recv_sem.at[k], line[AXES[k][1]][by])

    for k in range(3):
        wait_for(cp[k].at[0, pl.ds(0, 3)], w.sem_c1.at[k])
    lines_second_leg(cp, w.sem_c2s, w.sem_c2)
    second_leg(0, 0, 1)

    w.rem_t[...] = jnp.zeros((2 * NDEV, 8, V), F32)
    w.geo_t[:, 7, :] = jnp.ones((2 * NDEV, V), F32)
    w.en_all[mine] = jnp.zeros((2, V), F32)
    for i in range(3):
        wait_for(w.r1.at[i, pl.ds(0, 7)], w.sem_r.at[i])
    copy = pltpu.make_async_copy(w.r1, w.wanted, w.local_sem)
    copy.start()
    for k in range(3):
        i = DIMS.index(AXES[k][2])
        w.sel[k] = selection(k, jnp.concatenate([w.r1[i, d] for d in range(8)], axis=0))

    def ends(k):
        c = AXES[k][2]
        return [shifted(moved(c, by, o)) for by, o in ((2, 0), (2, 1), (1, 0), (1, 1), (3, 0), (3, 1), (0, 1))]

    def end_index(k, t):
        return t[AXES[k][2]] * 2 + t[1]

    for k in range(3):
        wait_for(cp[k].at[pl.ds(0, 3)], w.sem_c2.at[k])
        for g in range(1 + len(GEO[k])):
            source = cp[k][:, :, g].reshape(256, V)
            got = jnp.dot(w.sel[k], source, preferred_element_type=F32).astype(BF16)
            sg[k][:, g] = got.reshape(8, 32, V)
        me = end_index(k, here)
        rg[k][me] = sg[k][me]
        for to in ends(k):
            send(sg[k].at[end_index(k, to)], rg[k].at[me], w.sem_gs.at[0, k], w.sem_g.at[0, k], to)
    copy.wait()

    def first_leg_done(n):
        for k in range(3):
            wait_for(planes[n][k][0].at[pl.ds(0, 3)], w.sem_b1.at[n, k])
        second_leg(n, 1, 3)

    def spread(n, j):
        for k in range(3):
            a, b, c = AXES[k]
            wi = DIMS.index(c)
            plane = planes[n][k][j]
            if j:
                wait_for(plane, w.sem_b2.at[n, k, j])
            owners = []
            for i in range(4):
                t = list(here)
                t[a] = (here[a] + i) & 3
                t[b] = (here[b] + j) & 3
                owners.append((t, flat(t)))

            @pl.loop(0, 8)
            def _(d):
                for i, (t, o) in enumerate(owners):
                    for h in range(2):
                        w.ss[k, d, j, t[a], h] = plane[i, w.wanted[wi, d, h, o]]

            me = end_index(k, here)
            for i, (t, o) in enumerate(owners):
                for h in range(2):
                    block = plane[i, w.wanted[wi, me, h, o]]
                    tabs[n][t[0], t[1], t[2], t[3], h, SEG * k : SEG * (k + 1), :] = block
            at = list(owners[0][0])
            at[a] = slice(None)
            goal = tabs[n].at[at[0], at[1], at[2], at[3], :, pl.ds(SEG * k, SEG), :]
            for to in ends(k):
                send(w.ss.at[k, end_index(k, to), j], goal, w.sem_us.at[n, k], w.sem_u.at[n, k], to)

    def build(first, count, base):
        @pl.loop(0, SLOTS)
        def _(s):
            recv = receiver_features(w.geo[s])
            for jj in range(first // 2, (first + count) // 2):
                pair = [feats[base + idx[s, 2 * jj + i]] for i in range(2)]
                factors[s, jj] = pair_factors(jnp.concatenate(pair, axis=0), recv)

    def applied(load, s, first, count):
        total = None
        for jj in range(first // 2, (first + count) // 2):
            lhs = jnp.concatenate([load(idx[s, 2 * jj + i]) for i in range(2)], axis=1)
            term = jnp.dot(lhs, factors[s, jj], preferred_element_type=F32)
            total = term if total is None else total + term
        return total

    def near_apply():
        @pl.loop(0, SLOTS)
        def _(s):
            acc[s] = applied(lambda i: near_s[i], s, 0, NEAR)

    def far_apply(n):
        tab = tabs[n]
        r = rows_of((ROWS, V))
        mark = rows_of((2, V)) == n

        def load(i):
            head = tab[i >> 6, (i >> 5) & 1, (i >> 3) & 3, (i >> 1) & 3, i & 1]
            return jnp.concatenate([head, w.tail[i]], axis=0)

        @pl.loop(0, SLOTS)
        def _(s):
            total = acc[s] + applied(load, s, NEAR, FAR)
            a = [alb_ref[i, pl.ds(s, 1), :] for i in range(3)]
            total = total * jnp.where(r < 25, a[0], jnp.where(r < 50, a[1], a[2]))
            w.wide[:, s, :] = total
            if n == 0:
                value = total.astype(BF16)
                near_s[s] = value
                for k in range(3):
                    planes[1][k][0][0, s] = value[SEG * k : SEG * (k + 1)]
            energy = jnp.sum(total * total * area_ref[pl.ds(s, 1), :], axis=0, keepdims=True)
            w.en_all[mine] += jnp.where(mark, energy, 0.0)

    def tails(rows_of_part):
        for k in range(3):
            w.rem_t[:, k, :] = jnp.dot(canonical(k), rows_of_part(k), preferred_element_type=F32)
        w.tail[...] = w.rem_t[...].astype(BF16)

    first_leg_done(0)
    spread(0, 0)

    @pl.loop(0, SLOTS)
    def _(b):
        feats[2 * NDEV + b] = source_features(w.geo[b])

    build(0, NEAR, 2 * NDEV)
    for j in (1, 3, 2):
        spread(0, j)
    for k in range(3):
        wait_for(rg[k].at[pl.ds(0, 7)], w.sem_g.at[0, k])
        order = canonical(k)
        for g, comp in enumerate(GEO[k]):
            rows = rg[k][:, 1 + g].reshape(256, V)
            w.geo_t[:, comp, :] = jnp.dot(order, rows, preferred_element_type=F32)
    tails(lambda k: rg[k][:, 0].reshape(256, V))

    @pl.loop(0, 2 * NDEV)
    def _(b):
        feats[b] = source_features(w.geo_t[b])

    build(NEAR, FAR, 0)
    near_apply()
    for k in range(3):
        wait_for(w.ss.at[k, pl.ds(0, 7)], w.sem_u.at[0, k])
    far_apply(0)

    first_leg([p[0] for p in planes[1]], w.sem_b1s.at[1], w.sem_b1.at[1])
    second_leg(1, 0, 1)
    for k in range(3):
        w.cr[k, 0, 0] = w.wide[72 + k].astype(BF16)
    cr = [w.cr.at[k] for k in range(3)]
    first_leg([c.at[0] for c in cr], w.sem_r1s, w.sem_r1)
    b1_ref[...] = w.wide[:CH].astype(BF16)
    for k in range(3):
        wait_for(w.ss.at[k, pl.ds(0, 7)], w.sem_us.at[0, k])
    first_leg_done(1)
    spread(1, 0)
    for k in range(3):
        wait_for(cr[k].at[0, pl.ds(0, 3)], w.sem_r1.at[k])
    lines_second_leg(cr, w.sem_r2s, w.sem_r2)
    near_apply()
    for k in range(3):
        wait_for(cr[k].at[pl.ds(0, 3)], w.sem_r2.at[k])
        got = jnp.dot(w.sel[k], w.cr[k].reshape(256, V), preferred_element_type=F32).astype(BF16)
        w.sr[k] = got.reshape(8, 32, V)
        me = end_index(k, here)
        w.rr[k, me] = w.sr[k, me]
        for to in ends(k):
            send(w.sr.at[k, end_index(k, to)], w.rr.at[k, me], w.sem_gs.at[1, k], w.sem_g.at[1, k], to)
    for j in (1, 3, 2):
        spread(1, j)
    for k in range(3):
        wait_for(w.rr.at[k, pl.ds(0, 7)], w.sem_g.at[1, k])
    tails(lambda k: w.rr[k].reshape(256, V))
    for k in range(3):
        wait_for(w.ss.at[k, pl.ds(0, 7)], w.sem_u.at[1, k])
    far_apply(1)

    for off in ORDER:
        send(w.en_all.at[mine], w.en_all.at[mine], w.sem_e.at[0], w.sem_e.at[1], shifted(off))
    b2_ref[...] = w.wide[:CH].astype(BF16)
    wait_for(w.en_all.at[pl.ds(0, NDEV - 1)], w.sem_e.at[1])
    en_ref[...] = jnp.sum(w.en_all[...], axis=0)
    wait_for(w.en_all.at[pl.ds(0, NDEV - 1)], w.sem_e.at[0])
    for k in range(3):
        wait_for(w.r1.at[k, pl.ds(0, 7)], w.sem_rs.at[k])
        wait_for(cp[k].at[0, pl.ds(0, 3)], w.sem_c1s.at[k])
        wait_for(cp[k].at[pl.ds(0, 3)], w.sem_c2s.at[k])
        wait_for(cr[k].at[0, pl.ds(0, 3)], w.sem_r1s.at[k])
        wait_for(cr[k].at[pl.ds(0, 3)], w.sem_r2s.at[k])
        wait_for(rg[k].at[pl.ds(0, 7)], w.sem_gs.at[0, k])
        wait_for(w.rr.at[k, pl.ds(0, 7)], w.sem_gs.at[1, k])
        wait_for(w.ss.at[k, pl.ds(0, 7)], w.sem_us.at[1, k])
        for n in range(2):
            wait_for(planes[n][k][0].at[pl.ds(0, 3)], w.sem_b1s.at[n, k])
            for j in (1, 2, 3):
                wait_for(planes[n][k][j], w.sem_b2s.at[n, k])


def scratch_list():
    vm, dma = pltpu.VMEM, pltpu.SemaphoreType.DMA
    out = [
        ("r1", vm((3, 8, 2, V), I32)),
        ("wanted", pltpu.SMEM((3, 8, 2, V), I32)),
        ("near_s", vm((SLOTS, ROWS, V), BF16)),
        ("wide", vm((ROWS, SLOTS, V), F32)),
        ("geo", vm((SLOTS, 8, V), F32)),
        ("sel", vm((3, 256, 256), BF16)),
        ("cr", vm((3, 4, 4, SLOTS, V), BF16)),
        ("sr", vm((3, 8, 32, V), BF16)),
        ("rr", vm((3, 8, 32, V), BF16)),
        ("ss", vm((3, 8, 4, 4, 2, SEG, V), BF16)),
        ("tab_a", vm((4, 2, 4, 4, 2, 3 * SEG, V), BF16)),
        ("tab_b", vm((4, 2, 4, 4, 2, 3 * SEG, V), BF16)),
        ("geo_t", vm((2 * NDEV, 8, V), F32)),
        ("rem_t", vm((2 * NDEV, 8, V), F32)),
        ("tail", vm((2 * NDEV, 8, V), BF16)),
        ("feats", vm((2 * NDEV + SLOTS, 64, V), BF16)),
        ("factors", vm((SLOTS, (NEAR + FAR) // 2, 2 * V, V), BF16)),
        ("acc", vm((SLOTS, ROWS, V), F32)),
        ("en_all", vm((NDEV, 2, V), F32)),
        ("local_sem", dma),
        ("sem_e", dma((2,))),
        ("sem_b2", dma((2, 3, 4))),
    ]
    for k in range(3):
        size = 1 + len(GEO[k])
        out.append((f"cp{k}", vm((4, 4, size, SLOTS, V), BF16)))
        out.append((f"sg{k}", vm((8, size, 32, V), BF16)))
        out.append((f"rg{k}", vm((8, size, 32, V), BF16)))
        for n, j in itertools.product(range(2), range(4)):
            out.append((f"p{n}{k}{j}", vm((4, SLOTS, SEG, V), BF16)))
    for name in ("r", "rs", "c1", "c1s", "c2", "c2s", "r1", "r1s", "r2", "r2s"):
        out.append((f"sem_{name}", dma((3,))))
    for name in ("b1", "b1s", "b2s", "u", "us", "g", "gs"):
        out.append((f"sem_{name}", dma((2, 3))))
    return out


def body(transfer, positions, normals, area, albedo, pairs, home):
    vm = pl.BlockSpec(memory_space=pltpu.VMEM)
    sm = pl.BlockSpec(memory_space=pltpu.SMEM)
    idx, req = pl.pallas_call(
        index_kernel,
        out_shape=(jax.ShapeDtypeStruct((SLOTS, V), I32), jax.ShapeDtypeStruct((2, V), I32)),
        in_specs=[vm, vm],
        out_specs=(vm, vm),
        scratch_shapes=[pltpu.VMEM((SLOTS, V), I32)],
    )(pairs, home.reshape(16, V))
    major = lambda t: jnp.swapaxes(t, 0, 1)
    bounce = jax.ShapeDtypeStruct((CH, SLOTS, V), BF16)
    b1, b2, en = pl.pallas_call(
        main_kernel,
        out_shape=(bounce, bounce, jax.ShapeDtypeStruct((2, V), F32)),
        in_specs=[sm, vm, vm, vm, vm, vm, vm],
        out_specs=(vm, vm, vm),
        scratch_shapes=[shape for _, shape in scratch_list()],
        compiler_params=pltpu.CompilerParams(
            collective_id=0, has_side_effects=True, vmem_limit_bytes=62 * 2**20
        ),
    )(idx, req, major(transfer), major(positions), major(normals), area, major(albedo))
    energies = jnp.sum(en, axis=1) * (1.0 / (NDEV * SLOTS * CH * V))
    return major(b1), major(b2), energies


def solution(mesh):
    finer = Mesh(mesh.devices.reshape(SZ), AX)
    split = [P(AX, *([None] * n)) for n in (2, 2, 2, 1, 2, 1)]
    return jax.shard_map(
        body,
        mesh=finer,
        in_specs=(*split, P()),
        out_specs=(split[0], split[0], P()),
        check_vma=False,
    )
```

time: 195 us -> 135 us (0.69)
  Pallas kernels: 185 us -> 130 us
  local copies, waits for them, and re-layouts: 6.96 us -> 3.08 us
  other arithmetic: 2.7 us -> 0.63 us
    pallas_call x1, Pallas kernels: 183 us -> 129 us  [body(): pl.pallas_call(main_kernel, out_shape=(bounce, bounce, jax.ShapeDtypeStru...]
    unnamed x12 -> x6, local copies, waits for them, and re-layouts: 5.56 us -> 3.08 us
where the time goes in v2:
time: 135 us
  Pallas kernels  130 us (96%)
  local copies, waits for them, and re-layouts  3.08 us (2%)
    pallas_call x1, Pallas kernels, body(): pl.pallas_call(main_kernel, out_shape=(bounce, bounce, jax.ShapeDtypeStru...  129 us
    unnamed x6, local copies, waits for them, and re-layouts  3.08 us

profile of v2, /device:TPU:1, one launch (start us, length us, event | category | flops | bytes accessed | tf_op | source)
XLA Modules:
  0.0 134.8 jit_solution(5961786157993688214)
XLA Ops:
  0.6 1.7 %shard_map.94 = (s32[16,128]{1,0:T(8,128)}, s32[2,128]{1,0:T(2,128)}) custom-call(s32[16,40]{1,0:T(8,128)} %pairs_ref.1, s32[16,128]{1,0:T(8,128)} %bitcast.13), custom_call_target="tpu_custom_call" | custom-call | tf_op jit(solution)/shard_map/pallas_call | solution.py:497
  2.3 128.7 %shard_map.95 = (bf16[75,16,128]{2,1,0:T(8,128)(2,1)}, bf16[75,16,128]{2,1,0:T(8,128)(2,1)}, f32[2,128]{1,0:T(2,128)}) custom-call(s32[16,128]{1,0:T(8,128)} %get-tuple-element.8.idx, s32[2,128]{1,0:T(2,128)} %get-tuple-element.9.req_ref, bf16[75,16,128]{2,1,0:T(8,128)(2,1)} %bitcast.7, f32[3,16,128]{2,1,0:T(8,128)} %bitcast.10, f32[3,16,128]{2,1,0:T(8,128)} %bitcast.11, ...), custom_call_target="tpu_custom_call" | custom-call | tf_op jit(solution)/shard_map/pallas_call | solution.py:506
  131.0 0.0 copy-start.1
  131.1 0.6 copy-done.1
  131.7 0.1 reduce_sum.9
  131.8 0.5 broadcast_multiply_fusion
  132.3 0.0 copy-start
  132.3 1.7 %copy.12 = bf16[16,75,128]{2,0,1:T(8,128)(2,1)} copy(bf16[16,75,128]{2,0,1:T(8,128)(2,1)} %bitcast.9) | data formatting | bytes 614400
  134.0 0.0 copy-done
  134.0 0.7 copy.13
Async XLA Ops:
  131.0 0.6 copy-start.1
  132.3 1.8 %copy-start = (bf16[75,16,128]{2,1,0:T(8,128)(2,1)S(1)}, bf16[75,16,128]{2,1,0:T(8,128)(2,1)}, u32[]{:S(2)}) copy-start(bf16[75,16,128]{2,1,0:T(8,128)(2,1)} %get-tuple-element.11) | copy-start | bytes 921604

commit v3 on v2

--- a/solution.py
+++ b/solution.py
@@ -239,17 +239,34 @@
     first_leg([c.at[0] for c in cp], w.sem_c1s, w.sem_c1)
     first_leg([p[0] for p in planes[0]], w.sem_b1s.at[0], w.sem_b1.at[0])
 
+    def build(first, count, base, start, stop):
+        @pl.loop(start, stop)
+        def _(s):
+            recv = receiver_features(w.geo[s])
+            for jj in range(first // 2, (first + count) // 2):
+                pair = [feats[base + idx[s, 2 * jj + i]] for i in range(2)]
+                factors[s, jj] = pair_factors(jnp.concatenate(pair, axis=0), recv)
+
     def second_leg(n, part, size):
         for by in STEPS:
             for k in range(3):
                 send(planes[n][k][0].at[pl.ds(part, size)], planes[n][k][FROM[by]].at[pl.ds(part, size)],
                      w.sem_b2s.at[n, k], w.sem_b2.at[n, k, FROM[by]], line[AXES[k][1]][by])
 
+    def first_leg_done(n):
+        for k in range(3):
+            wait_for(planes[n][k][0].at[pl.ds(0, 3)], w.sem_b1.at[n, k])
+
     def lines_second_leg(refs, send_sem, recv_sem):
         for by in STEPS:
             for k in range(3):
                 send(refs[k].at[0], refs[k].at[FROM[by]], send_sem.at[k], recv_sem.at[k], line[AXES[k][1]][by])
 
+    @pl.loop(0, SLOTS)
+    def _(b):
+        feats[2 * NDEV + b] = source_features(w.geo[b])
+
+    build(0, NEAR, 2 * NDEV, 0, 8)
     for k in range(3):
         wait_for(cp[k].at[0, pl.ds(0, 3)], w.sem_c1.at[k])
     lines_second_leg(cp, w.sem_c2s, w.sem_c2)
@@ -265,6 +282,11 @@
     for k in range(3):
         i = DIMS.index(AXES[k][2])
         w.sel[k] = selection(k, jnp.concatenate([w.r1[i, d] for d in range(8)], axis=0))
+
+    build(0, NEAR, 2 * NDEV, 8, 12)
+    first_leg_done(0)
+    second_leg(0, 1, 1)
+    build(0, NEAR, 2 * NDEV, 12, SLOTS)
 
     def ends(k):
         c = AXES[k][2]
@@ -283,12 +305,6 @@
         rg[k][me] = sg[k][me]
         for to in ends(k):
             send(sg[k].at[end_index(k, to)], rg[k].at[me], w.sem_gs.at[0, k], w.sem_g.at[0, k], to)
-    copy.wait()
-
-    def first_leg_done(n):
-        for k in range(3):
-            wait_for(planes[n][k][0].at[pl.ds(0, 3)], w.sem_b1.at[n, k])
-        second_leg(n, 1, 3)
 
     def spread(n, j):
         for k in range(3):
@@ -321,14 +337,6 @@
             for to in ends(k):
                 send(w.ss.at[k, end_index(k, to), j], goal, w.sem_us.at[n, k], w.sem_u.at[n, k], to)
 
-    def build(first, count, base):
-        @pl.loop(0, SLOTS)
-        def _(s):
-            recv = receiver_features(w.geo[s])
-            for jj in range(first // 2, (first + count) // 2):
-                pair = [feats[base + idx[s, 2 * jj + i]] for i in range(2)]
-                factors[s, jj] = pair_factors(jnp.concatenate(pair, axis=0), recv)
-
     def applied(load, s, first, count):
         total = None
         for jj in range(first // 2, (first + count) // 2):
@@ -342,7 +350,7 @@
         def _(s):
             acc[s] = applied(lambda i: near_s[i], s, 0, NEAR)
 
-    def far_apply(n):
+    def far_apply(n, start, stop):
         tab = tabs[n]
         r = rows_of((ROWS, V))
         mark = rows_of((2, V)) == n
@@ -351,7 +359,7 @@
             head = tab[i >> 6, (i >> 5) & 1, (i >> 3) & 3, (i >> 1) & 3, i & 1]
             return jnp.concatenate([head, w.tail[i]], axis=0)
 
-        @pl.loop(0, SLOTS)
+        @pl.loop(start, stop)
         def _(s):
             total = acc[s] + applied(load, s, NEAR, FAR)
             a = [alb_ref[i, pl.ds(s, 1), :] for i in range(3)]
@@ -370,16 +378,9 @@
             w.rem_t[:, k, :] = jnp.dot(canonical(k), rows_of_part(k), preferred_element_type=F32)
         w.tail[...] = w.rem_t[...].astype(BF16)
 
-    first_leg_done(0)
+    second_leg(0, 2, 2)
+    copy.wait()
     spread(0, 0)
-
-    @pl.loop(0, SLOTS)
-    def _(b):
-        feats[2 * NDEV + b] = source_features(w.geo[b])
-
-    build(0, NEAR, 2 * NDEV)
-    for j in (1, 3, 2):
-        spread(0, j)
     for k in range(3):
         wait_for(rg[k].at[pl.ds(0, 7)], w.sem_g.at[0, k])
         order = canonical(k)
@@ -392,26 +393,40 @@
     def _(b):
         feats[b] = source_features(w.geo_t[b])
 
-    build(NEAR, FAR, 0)
+    build(NEAR, FAR, 0, 0, 6)
+    for j in (1, 3, 2):
+        spread(0, j)
+    build(NEAR, FAR, 0, 6, SLOTS)
     near_apply()
     for k in range(3):
         wait_for(w.ss.at[k, pl.ds(0, 7)], w.sem_u.at[0, k])
-    far_apply(0)
-
-    first_leg([p[0] for p in planes[1]], w.sem_b1s.at[1], w.sem_b1.at[1])
-    second_leg(1, 0, 1)
+
+    def half_leg(start):
+        part = pl.ds(start, SLOTS // 2)
+        for by in STEPS:
+            for k in range(3):
+                line0 = planes[1][k][0]
+                send(line0.at[0, part], line0.at[FROM[by], part],
+                     w.sem_b1s.at[1, k], w.sem_b1.at[1, k], line[AXES[k][0]][by])
+
+    far_apply(0, 0, SLOTS // 2)
+    half_leg(0)
+    far_apply(0, SLOTS // 2, SLOTS)
     for k in range(3):
         w.cr[k, 0, 0] = w.wide[72 + k].astype(BF16)
     cr = [w.cr.at[k] for k in range(3)]
     first_leg([c.at[0] for c in cr], w.sem_r1s, w.sem_r1)
+    half_leg(SLOTS // 2)
+    second_leg(1, 0, 1)
     b1_ref[...] = w.wide[:CH].astype(BF16)
     for k in range(3):
         wait_for(w.ss.at[k, pl.ds(0, 7)], w.sem_us.at[0, k])
-    first_leg_done(1)
-    spread(1, 0)
     for k in range(3):
         wait_for(cr[k].at[0, pl.ds(0, 3)], w.sem_r1.at[k])
     lines_second_leg(cr, w.sem_r2s, w.sem_r2)
+    first_leg_done(1)
+    second_leg(1, 1, 3)
+    spread(1, 0)
     near_apply()
     for k in range(3):
         wait_for(cr[k].at[pl.ds(0, 3)], w.sem_r2.at[k])
@@ -428,7 +443,7 @@
     tails(lambda k: w.rr[k].reshape(256, V))
     for k in range(3):
         wait_for(w.ss.at[k, pl.ds(0, 7)], w.sem_u.at[1, k])
-    far_apply(1)
+    far_apply(1, 0, SLOTS)
 
     for off in ORDER:
         send(w.en_all.at[mine], w.en_all.at[mine], w.sem_e.at[0], w.sem_e.at[1], shifted(off))
@@ -449,6 +464,13 @@
             wait_for(planes[n][k][0].at[pl.ds(0, 3)], w.sem_b1s.at[n, k])
             for j in (1, 2, 3):
                 wait_for(planes[n][k][j], w.sem_b2s.at[n, k])
+
+
+def last_kernel(b1_ref, b2_ref, en_ref, o1_ref, o2_ref, sum_ref):
+    o1_ref[...] = b1_ref[...]
+    o2_ref[...] = b2_ref[...]
+    for i in range(2):
+        sum_ref[i] = jnp.sum(en_ref[i : i + 1, :]) * (1.0 / (NDEV * SLOTS * CH * V))
 
 
 def scratch_list():
@@ -513,7 +535,12 @@
             collective_id=0, has_side_effects=True, vmem_limit_bytes=62 * 2**20
         ),
     )(idx, req, major(transfer), major(positions), major(normals), area, major(albedo))
-    energies = jnp.sum(en, axis=1) * (1.0 / (NDEV * SLOTS * CH * V))
+    b1, b2, energies = pl.pallas_call(
+        last_kernel,
+        out_shape=(bounce, bounce, jax.ShapeDtypeStruct((2,), F32)),
+        in_specs=[vm, vm, vm],
+        out_specs=(vm, vm, sm),
+    )(b1, b2, en)
     return major(b1), major(b2), energies
 
 

time: 135 us -> 124 us (0.919)
  Pallas kernels: 130 us -> 123 us
  local copies, waits for them, and re-layouts: 3.08 us -> 0 us
    pallas_call x1, Pallas kernels: 129 us -> 119 us  [body(): pl.pallas_call(main_kernel, out_shape=(bounce, bounce, jax.ShapeDtypeStru...]
    unnamed x6 -> x0, local copies, waits for them, and re-layouts: 3.08 us -> none
    pallas_call x0 -> x1, Pallas kernels: none -> 1.91 us  [body(): pl.pallas_call(last_kernel, out_shape=(bounce, bounce, jax.ShapeDtypeStru...]
where the time goes in v3:
time: 124 us
  Pallas kernels  123 us (99%)
    pallas_call x1, Pallas kernels, body(): pl.pallas_call(main_kernel, out_shape=(bounce, bounce, jax.ShapeDtypeStru...  119 us

profile of v3, /device:TPU:1, one launch (start us, length us, event | category | flops | bytes accessed | tf_op | source)
XLA Modules:
  0.0 123.6 jit_solution(14636793628292543889)
XLA Ops:
  0.6 1.7 %shard_map.94 = (s32[16,128]{1,0:T(8,128)}, s32[2,128]{1,0:T(2,128)}) custom-call(s32[16,40]{1,0:T(8,128)} %pairs_ref.1, s32[16,128]{1,0:T(8,128)} %bitcast.11), custom_call_target="tpu_custom_call" | custom-call | tf_op jit(solution)/shard_map/pallas_call | solution.py:519
  2.3 119.4 %shard_map.95 = (bf16[75,16,128]{2,1,0:T(8,128)(2,1)}, bf16[75,16,128]{2,1,0:T(8,128)(2,1)}, f32[2,128]{1,0:T(2,128)}) custom-call(s32[16,128]{1,0:T(8,128)} %get-tuple-element.11.idx, s32[2,128]{1,0:T(2,128)} %get-tuple-element.12.req_ref, bf16[75,16,128]{2,1,0:T(8,128)(2,1)} %bitcast.7, f32[3,16,128]{2,1,0:T(8,128)} %bitcast.8, f32[3,16,128]{2,1,0:T(8,128)} %bitcast.9, ...), custom_call_target="tpu_custom_call" | custom-call | tf_op jit(solution)/shard_map/pallas_call | solution.py:528
  121.7 1.9 %shard_map.96 = (bf16[75,16,128]{2,1,0:T(8,128)(2,1)}, bf16[75,16,128]{2,1,0:T(8,128)(2,1)}, f32[2]{0:T(128)}) custom-call(bf16[75,16,128]{2,1,0:T(8,128)(2,1)} %get-tuple-element.13.b1_ref, bf16[75,16,128]{2,1,0:T(8,128)(2,1)} %get-tuple-element.14.b2_ref, f32[2,128]{1,0:T(2,128)} %get-tuple-element.15.en_ref), custom_call_target="tpu_custom_call" | custom-call | tf_op jit(solution)/shard_map/pallas_call | solution.py:538

commit v4 on v3

--- a/solution.py
+++ b/solution.py
@@ -248,7 +248,7 @@
                 factors[s, jj] = pair_factors(jnp.concatenate(pair, axis=0), recv)
 
     def second_leg(n, part, size):
-        for by in STEPS:
+        for by in (1, 3):
             for k in range(3):
                 send(planes[n][k][0].at[pl.ds(part, size)], planes[n][k][FROM[by]].at[pl.ds(part, size)],
                      w.sem_b2s.at[n, k], w.sem_b2.at[n, k, FROM[by]], line[AXES[k][1]][by])
@@ -306,12 +306,21 @@
         for to in ends(k):
             send(sg[k].at[end_index(k, to)], rg[k].at[me], w.sem_gs.at[0, k], w.sem_g.at[0, k], to)
 
+    def relay(n):
+        for j, by, start in ((1, 3, 0), (3, 1, 2)):
+            part = pl.ds(start, 2)
+            for k in range(3):
+                plane = planes[n][k][j]
+                wait_for(plane, w.sem_b2.at[n, k, j])
+                send(plane.at[part], planes[n][k][2].at[part],
+                     w.sem_b2s.at[n, k], w.sem_b2.at[n, k, 2], line[AXES[k][1]][by])
+
     def spread(n, j):
         for k in range(3):
             a, b, c = AXES[k]
             wi = DIMS.index(c)
             plane = planes[n][k][j]
-            if j:
+            if j == 2:
                 wait_for(plane, w.sem_b2.at[n, k, j])
             owners = []
             for i in range(4):
@@ -346,9 +355,10 @@
         return total
 
     def near_apply():
-        @pl.loop(0, SLOTS)
-        def _(s):
-            acc[s] = applied(lambda i: near_s[i], s, 0, NEAR)
+        @pl.loop(0, SLOTS // 2)
+        def _(p):
+            for s in (2 * p, 2 * p + 1):
+                acc[s] = applied(lambda i: near_s[i], s, 0, NEAR)
 
     def far_apply(n, start, stop):
         tab = tabs[n]
@@ -359,19 +369,20 @@
             head = tab[i >> 6, (i >> 5) & 1, (i >> 3) & 3, (i >> 1) & 3, i & 1]
             return jnp.concatenate([head, w.tail[i]], axis=0)
 
-        @pl.loop(start, stop)
-        def _(s):
-            total = acc[s] + applied(load, s, NEAR, FAR)
-            a = [alb_ref[i, pl.ds(s, 1), :] for i in range(3)]
-            total = total * jnp.where(r < 25, a[0], jnp.where(r < 50, a[1], a[2]))
-            w.wide[:, s, :] = total
-            if n == 0:
-                value = total.astype(BF16)
-                near_s[s] = value
-                for k in range(3):
-                    planes[1][k][0][0, s] = value[SEG * k : SEG * (k + 1)]
-            energy = jnp.sum(total * total * area_ref[pl.ds(s, 1), :], axis=0, keepdims=True)
-            w.en_all[mine] += jnp.where(mark, energy, 0.0)
+        @pl.loop(start // 2, stop // 2)
+        def _(p):
+            both = [(s, applied(load, s, NEAR, FAR)) for s in (2 * p, 2 * p + 1)]
+            for s, far in both:
+                a = [alb_ref[i, pl.ds(s, 1), :] for i in range(3)]
+                total = (acc[s] + far) * jnp.where(r < 25, a[0], jnp.where(r < 50, a[1], a[2]))
+                w.wide[:, s, :] = total
+                if n == 0:
+                    value = total.astype(BF16)
+                    near_s[s] = value
+                    for k in range(3):
+                        planes[1][k][0][0, s] = value[SEG * k : SEG * (k + 1)]
+                energy = jnp.sum(total * total * area_ref[pl.ds(s, 1), :], axis=0, keepdims=True)
+                w.en_all[mine] += jnp.where(mark, energy, 0.0)
 
     def tails(rows_of_part):
         for k in range(3):
@@ -393,9 +404,11 @@
     def _(b):
         feats[b] = source_features(w.geo_t[b])
 
+    relay(0)
+    spread(0, 1)
+    spread(0, 3)
     build(NEAR, FAR, 0, 0, 6)
-    for j in (1, 3, 2):
-        spread(0, j)
+    spread(0, 2)
     build(NEAR, FAR, 0, 6, SLOTS)
     near_apply()
     for k in range(3):
@@ -436,6 +449,7 @@
         w.rr[k, me] = w.sr[k, me]
         for to in ends(k):
             send(w.sr.at[k, end_index(k, to)], w.rr.at[k, me], w.sem_gs.at[1, k], w.sem_g.at[1, k], to)
+    relay(1)
     for j in (1, 3, 2):
         spread(1, j)
     for k in range(3):

time: 124 us -> 111 us (0.90)
  Pallas kernels: 123 us -> 110 us
    pallas_call x1, Pallas kernels: 119 us -> 106 us  [body(): pl.pallas_call(main_kernel, out_shape=(bounce, bounce, jax.ShapeDtypeStru...]
where the time goes in v4:
time: 111 us
  Pallas kernels  110 us (99%)
    pallas_call x1, Pallas kernels, body(): pl.pallas_call(main_kernel, out_shape=(bounce, bounce, jax.ShapeDtypeStru...  106 us

profile of v4, /device:TPU:1, one launch (start us, length us, event | category | flops | bytes accessed | tf_op | source)
XLA Modules:
  0.0 110.5 jit_solution(2610231638695005717)
XLA Ops:
  0.6 1.7 %shard_map.94 = (s32[16,128]{1,0:T(8,128)}, s32[2,128]{1,0:T(2,128)}) custom-call(s32[16,40]{1,0:T(8,128)} %pairs_ref.1, s32[16,128]{1,0:T(8,128)} %bitcast.11), custom_call_target="tpu_custom_call" | custom-call | tf_op jit(solution)/shard_map/pallas_call | solution.py:533
  2.3 106.3 %shard_map.95 = (bf16[75,16,128]{2,1,0:T(8,128)(2,1)}, bf16[75,16,128]{2,1,0:T(8,128)(2,1)}, f32[2,128]{1,0:T(2,128)}) custom-call(s32[16,128]{1,0:T(8,128)} %get-tuple-element.11.idx, s32[2,128]{1,0:T(2,128)} %get-tuple-element.12.req_ref, bf16[75,16,128]{2,1,0:T(8,128)(2,1)} %bitcast.7, f32[3,16,128]{2,1,0:T(8,128)} %bitcast.8, f32[3,16,128]{2,1,0:T(8,128)} %bitcast.9, ...), custom_call_target="tpu_custom_call" | custom-call | tf_op jit(solution)/shard_map/pallas_call | solution.py:542
  108.6 1.9 %shard_map.96 = (bf16[75,16,128]{2,1,0:T(8,128)(2,1)}, bf16[75,16,128]{2,1,0:T(8,128)(2,1)}, f32[2]{0:T(128)}) custom-call(bf16[75,16,128]{2,1,0:T(8,128)(2,1)} %get-tuple-element.13.b1_ref, bf16[75,16,128]{2,1,0:T(8,128)(2,1)} %get-tuple-element.14.b2_ref, f32[2,128]{1,0:T(2,128)} %get-tuple-element.15.en_ref), custom_call_target="tpu_custom_call" | custom-call | tf_op jit(solution)/shard_map/pallas_call | solution.py:552

commit v5 on v4

--- a/solution.py
+++ b/solution.py
@@ -392,6 +392,7 @@
     second_leg(0, 2, 2)
     copy.wait()
     spread(0, 0)
+    near_apply()
     for k in range(3):
         wait_for(rg[k].at[pl.ds(0, 7)], w.sem_g.at[0, k])
         order = canonical(k)
@@ -410,7 +411,6 @@
     build(NEAR, FAR, 0, 0, 6)
     spread(0, 2)
     build(NEAR, FAR, 0, 6, SLOTS)
-    near_apply()
     for k in range(3):
         wait_for(w.ss.at[k, pl.ds(0, 7)], w.sem_u.at[0, k])
 

time: 111 us -> 110 us (level)
    pallas_call x1, Pallas kernels: 106 us -> 105 us  [body(): pl.pallas_call(main_kernel, out_shape=(bounce, bounce, jax.ShapeDtypeStru...]
where the time goes in v5:
time: 110 us; the launch traced here: 109 us
  Pallas kernels  109 us (99%)
    pallas_call x1, Pallas kernels, body(): pl.pallas_call(main_kernel, out_shape=(bounce, bounce, jax.ShapeDtypeStru...  105 us

profile of v5, /device:TPU:1, one launch (start us, length us, event | category | flops | bytes accessed | tf_op | source)
XLA Modules:
  0.0 109.4 jit_solution(7483915304283545038)
XLA Ops:
  0.6 1.7 %shard_map.94 = (s32[16,128]{1,0:T(8,128)}, s32[2,128]{1,0:T(2,128)}) custom-call(s32[16,40]{1,0:T(8,128)} %pairs_ref.1, s32[16,128]{1,0:T(8,128)} %bitcast.11), custom_call_target="tpu_custom_call" | custom-call | tf_op jit(solution)/shard_map/pallas_call | solution.py:533
  2.3 105.1 %shard_map.95 = (bf16[75,16,128]{2,1,0:T(8,128)(2,1)}, bf16[75,16,128]{2,1,0:T(8,128)(2,1)}, f32[2,128]{1,0:T(2,128)}) custom-call(s32[16,128]{1,0:T(8,128)} %get-tuple-element.11.idx, s32[2,128]{1,0:T(2,128)} %get-tuple-element.12.req_ref, bf16[75,16,128]{2,1,0:T(8,128)(2,1)} %bitcast.7, f32[3,16,128]{2,1,0:T(8,128)} %bitcast.8, f32[3,16,128]{2,1,0:T(8,128)} %bitcast.9, ...), custom_call_target="tpu_custom_call" | custom-call | tf_op jit(solution)/shard_map/pallas_call | solution.py:542
  107.5 1.9 %shard_map.96 = (bf16[75,16,128]{2,1,0:T(8,128)(2,1)}, bf16[75,16,128]{2,1,0:T(8,128)(2,1)}, f32[2]{0:T(128)}) custom-call(bf16[75,16,128]{2,1,0:T(8,128)(2,1)} %get-tuple-element.13.b1_ref, bf16[75,16,128]{2,1,0:T(8,128)(2,1)} %get-tuple-element.14.b2_ref, f32[2,128]{1,0:T(2,128)} %get-tuple-element.15.en_ref), custom_call_target="tpu_custom_call" | custom-call | tf_op jit(solution)/shard_map/pallas_call | solution.py:552
